TPU v7x, 256 devices: a 8x8x2 block of a 8x8x16 slice. The times are simulated.
256 devices in a mesh: groups: 2 (over z), seq: 128 (over x, y, core).
Axes of the slice: x: 8, y: 8, z: 2, core: 2. Of those that a mesh axis runs over, the one named last changes fastest.
The devices are a block of a 8x8x16 slice.
Arguments:
- hidden_in: bfloat16 [8, 4096], P('groups', 'seq'), parts along dimension 0, may hold values from -2 to 2
- in_gain: float32 [4096], replicated, may hold values from 0.5 to 1.5
- qkv_weight: bfloat16 [4096, 9216], P(None, 'seq'), may hold values from -0.09375 to 0.09375
- q_gain: float32 [128], replicated, may hold values from 0.25 to 1.75
- k_cache: bfloat16 [8, 131072, 128], P('groups', 'seq'), parts along dimension 0, may hold values from -600 to 600
- v_cache: bfloat16 [8, 131072, 128], P('groups', 'seq'), parts along dimension 0, may hold values from -6 to 6
- lengths: int32 [8], P('groups'), parts along dimension 0, may hold values from 16384 to 32768
- out_weight: bfloat16 [4, 2048, 4096], P(None, 'seq'), may hold values from -0.25 to 0.25
- post_gain: float32 [4096], replicated, may hold values from 0.5 to 1.5
- gate_weight: bfloat16 [128, 4096, 384], P('seq'), may hold values from -0.09375 to 0.09375
- up_weight: bfloat16 [128, 4096, 384], P('seq'), may hold values from -0.09375 to 0.09375
- down_weight: bfloat16 [128, 384, 4096], P('seq'), may hold values from -0.875 to 0.875
- expert_ids: int32 [8, 8], P('groups'), parts along dimension 0, may hold values from 0 to 63, as said below
- route_weight: float32 [8, 8], P('groups'), parts along dimension 0, may hold values from 0.25 to 4
Outputs:
- mixed: float32 [8, 4096], P('groups', 'seq'), parts along dimension 0
There are 2 independent parts, one for each index of `groups`. A program takes and returns all parts, laid end to end along the dimension named above; an argument that names none is the same for every part. Nothing has to cross between parts.
Inputs may be any that keep to these rules, and one draw needn't show every extreme that they name: `expert_ids`: each row names 8 different experts.
All inputs are finite; a program needn't handle non-finite values.
Results may differ from a plain program's by a relative error of at most 0.017.
Values may be sent and summed in bfloat16 or wider, within the bound.
A program may use at most 64 MiB of HBM per device.

v0:
```python
import jax
import jax.numpy as jnp
from jax import lax
from jax.sharding import Mesh
from jax.sharding import PartitionSpec as P

HEADS = 64
KVH = 4
HD = 128
SEQ = ("seq_0", "seq_1", "seq_2")


EPSILON = 1e-06
ROPE_BASE = 1000000.0


def gathered_once(shard, axis):
    leaves = jax.tree.leaves(shard)
    order = sorted(range(len(leaves)), key=lambda k: -leaves[k].size)
    width = (1, *leaves[order[0]].shape)[-1]
    lines = [
        jnp.pad(leaves[k].reshape(-1), (0, -leaves[k].size % width)).reshape(-1, width)
        for k in order
    ]
    both, at, found = (lax.all_gather(jnp.concatenate(lines), axis), 0, {})
    for k, line in zip(order, lines):
        piece = both[:, at : at + len(line)].reshape(len(both), -1)
        found[k] = piece[:, : leaves[k].size].reshape(-1, *leaves[k].shape)
        at += len(line)
    numbers = iter(range(len(leaves)))
    return jax.tree.map(lambda _: found[next(numbers)], shard)


def combined_by_axis(shard, axes, combine):
    for axis in axes:
        pieces = gathered_once(shard, axis)
        shard = jax.tree.map(lambda part: part[0], pieces)
        for k in range(1, lax.axis_size(axis)):
            shard = combine(shard, jax.tree.map(lambda part: part[k], pieces))
    return shard


def over_pieces(shard, axis):
    pieces = lax.all_gather(shard, axis)
    return pieces.sum(axis=0)


def reduced_to_own(pieces, axes, order):
    inside = pieces.shape[1:]
    pieces = pieces.reshape(*(lax.axis_size(a) for a in axes), *inside)
    pieces = jnp.moveaxis(pieces, order, range(len(axes))).reshape(-1, *inside)
    for k in order:
        pieces = lax.psum_scatter(pieces, axes[k], scatter_dimension=0, tiled=True)
    return pieces[0]


def split_up(shard, dim, length):
    shape = shard.shape
    pieces = shard.reshape(*shape[:dim], length, shape[dim] // length, *shape[dim + 1 :])
    return jnp.moveaxis(pieces, dim, 0)


def sum_by_axis(shard, axes, order, dim):
    length = lax.axis_size(axes)
    return reduced_to_own(split_up(shard, dim, length), axes, order)


def rms_scale(values, gain_vec):
    mean_square = jnp.mean(values * values, axis=-1, keepdims=True)
    return values * lax.rsqrt(mean_square + EPSILON) * gain_vec


def rotate(values, positions):
    half_dim = values.shape[-1] // 2
    frequency = ROPE_BASE ** (-(2.0 * jnp.arange(half_dim, dtype=jnp.float32)) / values.shape[-1])
    angles = positions.astype(jnp.float32)[:, None] * frequency[None, :]
    cosine = jnp.cos(angles)[:, None, :]
    sine_vals = jnp.sin(angles)[:, None, :]
    lower_half = values[..., :half_dim]
    upper_half = values[..., half_dim:]
    return jnp.concatenate(
        [
            lower_half * cosine - upper_half * sine_vals,
            upper_half * cosine + lower_half * sine_vals,
        ],
        axis=-1,
    )


def project_heads(qkv_all, lengths, q_gain):
    seq_count = qkv_all.shape[0]
    query_cols = HEADS * HD
    key_cols = KVH * HD
    q_raw = qkv_all[:, :query_cols].astype(jnp.float32).reshape(seq_count, HEADS, HD)
    k_raw = (
        qkv_all[:, query_cols : query_cols + key_cols]
        .astype(jnp.float32)
        .reshape(seq_count, KVH, HD)
    )
    value_new = qkv_all[:, query_cols + key_cols :].reshape(seq_count, KVH, HD)
    queries = (rotate(rms_scale(q_raw, q_gain), lengths) * HD ** (-0.5)).astype(jnp.bfloat16)
    queries = queries.reshape(seq_count, KVH, HEADS // KVH, HD)
    key_new = rotate(rms_scale(k_raw, 1.0), lengths).astype(jnp.bfloat16)
    return (queries, key_new, value_new)


def merge_states(earlier, later):
    first_top, first_total, first_out = earlier
    second_top, second_total, second_out = later
    highest = jnp.maximum(first_top, second_top)
    first_scale = jnp.exp(first_top - highest)
    second_scale = jnp.exp(second_top - highest)
    merged_total = first_scale * first_total + second_scale * second_total
    merged_out = first_scale[..., None] * first_out + second_scale[..., None] * second_out
    return (highest, merged_total, merged_out)


def on_device(
    hidden_in,
    in_gain,
    qkv_weight,
    q_gain,
    k_cache,
    v_cache,
    lengths,
    out_weight,
    post_gain,
    gate_weight,
    up_weight,
    down_weight,
    expert_ids,
    route_weight,
):
    devices = lax.axis_size(SEQ)
    dev_index = lax.axis_index(SEQ)
    seq_count = hidden_in.shape[0]
    rows_local = k_cache.shape[1]
    width_local = hidden_in.shape[1]
    group_size = devices // KVH
    head_group = dev_index // group_size
    block_index = dev_index % group_size
    piece = HEADS * HD // (KVH * devices)
    whole_x = lax.all_gather(hidden_in, SEQ, axis=1, tiled=True)
    normed = rms_scale(whole_x.astype(jnp.float32), in_gain).astype(jnp.bfloat16)
    local_qkv = jnp.dot(normed, qkv_weight, preferred_element_type=jnp.float32).astype(jnp.bfloat16)
    qkv_all = lax.all_gather(local_qkv, SEQ, axis=1, tiled=True)
    queries, key_new, value_new = project_heads(qkv_all, lengths, q_gain)
    own_score = jnp.einsum("sgjd,sgd->sgj", queries, key_new, preferred_element_type=jnp.float32)
    query_local = lax.dynamic_index_in_dim(queries, head_group, 1, keepdims=False)
    positions = block_index * rows_local + jnp.arange(rows_local, dtype=jnp.int32)
    live_mask = (positions[None, :] < lengths[:, None])[:, None, :]
    scores = jnp.einsum("sjd,scd->sjc", query_local, k_cache, preferred_element_type=jnp.float32)
    scores = jnp.where(live_mask, scores, -1e30)
    row_top = jnp.max(scores, axis=-1)
    exp_scores = jnp.where(live_mask, jnp.exp(scores - row_top[..., None]), 0.0)
    row_total = jnp.sum(exp_scores, axis=-1)
    local_out = jnp.einsum(
        "sjc,scd->sjd", exp_scores.astype(jnp.bfloat16), v_cache, preferred_element_type=jnp.float32
    )
    selector = (jnp.arange(KVH, dtype=jnp.int32) == head_group)[None, :, None]
    value_wide = value_new.astype(jnp.float32)[:, :, None, :]
    tops_full = jnp.where(selector, row_top[:, None, :], -1e30)
    totals_full = jnp.where(selector, row_total[:, None, :], 0.0)
    outs_full = jnp.where(selector[..., None], local_out[:, None, :, :], 0.0)
    merged_top, merged_total, merged_out = combined_by_axis(
        (tops_full, totals_full, outs_full), SEQ, merge_states
    )
    highest = jnp.maximum(merged_top, own_score)
    block_scale = jnp.exp(merged_top - highest)
    own_weight = jnp.exp(own_score - highest)
    total_all = block_scale * merged_total + own_weight
    summed = block_scale[..., None] * merged_out + own_weight[..., None] * value_wide
    attn_part = lax.dynamic_index_in_dim(
        (summed / total_all[..., None]).reshape(seq_count, KVH, devices, piece),
        dev_index,
        2,
        keepdims=False,
    ).astype(jnp.bfloat16)
    proj_terms = jnp.einsum(
        "sgp,gpd->sd", attn_part, out_weight, preferred_element_type=jnp.float32
    )
    first_col = dev_index * width_local
    proj_whole = over_pieces(proj_terms, SEQ)
    resid_whole = whole_x.astype(jnp.float32) + proj_whole
    post = rms_scale(resid_whole, post_gain).astype(jnp.bfloat16)
    resid_part = lax.dynamic_slice_in_dim(resid_whole, first_col, width_local, 1)
    gate_val = jnp.dot(post, gate_weight[0], preferred_element_type=jnp.float32)
    up_val = jnp.dot(post, up_weight[0], preferred_element_type=jnp.float32)
    activated = (jax.nn.silu(gate_val) * up_val).astype(jnp.bfloat16)
    slab_out = jnp.dot(activated, down_weight[0], preferred_element_type=jnp.float32)
    route = route_weight / jnp.sum(route_weight, axis=-1, keepdims=True)
    route_coef = jnp.sum(jnp.where(expert_ids == dev_index // 2, route, 0.0), axis=-1)
    moe_part = sum_by_axis(route_coef[:, None] * slab_out, SEQ, (2, 0, 1), 1)
    return resid_part + moe_part


def solution(mesh):
    split = Mesh(
        mesh.devices.reshape(mesh.shape["groups"], 8, 8, 2), ("groups", "seq_0", "seq_1", "seq_2")
    )
    placed = (
        P("groups", SEQ),
        P(),
        P(None, SEQ),
        P(),
        P("groups", SEQ, None),
        P("groups", SEQ, None),
        P("groups"),
        P(None, SEQ, None),
        P(),
        P(SEQ, None, None),
        P(SEQ, None, None),
        P(SEQ, None, None),
        P("groups", None),
        P("groups", None),
    )
    return jax.shard_map(
        on_device, mesh=split, in_specs=placed, out_specs=P("groups", SEQ), check_vma=False
    )
```

profile of v0, /device:TPU:516, one launch (start us, length us, event | category | flops | bytes accessed | tf_op | source)
XLA Modules:
  0.0 434.9 jit_solution(10990292245268557305)
XLA Ops:
  6.6 0.8 convert_element_type.49
  7.4 0.8 broadcast_compare_fusion
  8.2 62.8 %all-gather.4 = bf16[128,32,4]{1,2,0:T(4,128)(2,1)S(1)} all-gather(bf16[1,32,4]{1,2,0:T(4,128)(2,1)} %bitcast.779), channel_id=1, replica_groups=mesh['groups'=2,'seq_0'=8,'seq_1'=8,'seq_2'=2] {'seq_0','seq_1','seq_2'}, dimensions={0}, use_global_device_ids=true | all-gather | bytes 33024 | tf_op jit(solution)/shard_map/all_gather | solution.py:143
  71.2 0.8 copy.48
  72.0 1.1 reshape.1049
  73.2 1.4 fusion.11
  74.6 50.7 %all-gather.5 = bf16[128,72,4]{1,2,0:T(4,128)(2,1)S(1)} all-gather(bf16[1,72,4]{1,2,0:T(4,128)(2,1)S(1)} %fusion.11), channel_id=1, replica_groups=mesh['groups'=2,'seq_0'=8,'seq_1'=8,'seq_2'=2] {'seq_0','seq_1','seq_2'}, dimensions={0}, use_global_device_ids=true | all-gather | bytes 74304 | tf_op jit(solution)/shard_map/all_gather | solution.py:146
  125.7 0.8 fusion.19
  126.8 1.7 fusion.168
  128.7 1.5 fusion.16
  131.6 39.5 %all-gather.14.cloned.1.call-done = f32[8,260,128]{2,1,0:T(8,128)} async-done(((f32[1,260,128]{2,1,0:T(8,128)}), f32[8,260,128]{2,1,0:T(8,128)}) %all-gather.14.cloned.1.call-update) | async-done | bytes 1064976 | tf_op jit(solution)/shard_map/all_gather | solution.py:25
  171.1 0.8 fusion.86
  171.9 0.8 bitcast_maximum_fusion.13
  172.6 0.9 fusion.112
  173.5 0.8 subtract_exponential_fusion.11
  174.3 1.8 fusion.42
  177.0 1.3 mul.759
  178.8 38.1 %all-gather.16.cloned.1.call-done = f32[8,260,128]{2,1,0:T(8,128)} async-done(((f32[1,260,128]{2,1,0:T(8,128)}), f32[8,260,128]{2,1,0:T(8,128)}) %all-gather.16.cloned.1.call-update) | async-done | bytes 1064976 | tf_op jit(solution)/shard_map/all_gather | solution.py:25
  217.0 0.8 fusion.88
  217.7 0.8 bitcast_maximum_fusion
  218.5 0.9 fusion.91
  219.4 0.8 subtract_exponential_fusion.6
  220.2 1.8 fusion.21
  222.0 2.1 all-gather.8
  225.3 1.0 mul.747
  226.3 0.7 mul.750
  227.0 1.0 mul.751
  228.0 0.7 mul.743
  228.8 1.0 mul.744
  230.5 1.0 mul.756
  232.3 1.0 div.68
  233.3 1.3 squeeze.279
  234.7 0.8 constant_dynamic-slice_fusion.5
  235.7 1.3 squeeze.280
  237.0 0.9 constant_dynamic-slice_fusion
  238.0 0.8 copy.60
  239.0 1.0 divide_convert_fusion
  240.2 1.9 convolution_bitcast_fusion
  242.8 82.5 %all-gather.18.cloned.1.call-done = f32[128,4,4096]{2,1,0:T(4,128)} async-done(((f32[1,4,4096]{2,1,0:T(4,128)}), f32[128,4,4096]{2,1,0:T(4,128)}) %all-gather.18.cloned.1.call-update) | async-done | bytes 8388624 | tf_op jit(solution)/shard_map/all_gather | solution.py:44
  325.3 4.6 %reduce_sum.76 = f32[4,4096]{1,0:T(4,128)S(1)} reduce(f32[128,4,4096]{2,1,0:T(4,128)} %all-gather.18.cloned.1.call-done, f32[]{:T(128)} %constant.82.clone.1), dimensions={0}, to_apply=%region_5.6 | reduce | flops 2080768 | bytes 8454148 | tf_op jit(solution)/shard_map/reduce_sum | solution.py:45
  330.0 2.4 fusion.3
  332.5 3.2 convolution_multiply_fusion
  335.9 0.9 copy.54
  339.8 26.4 %all-reduce.5.cloned.1.call-done = f32[128,4,32]{2,1,0:T(4,128)} async-done(((f32[128,4,32]{2,1,0:T(4,128)}), f32[128,4,32]{2,1,0:T(4,128)}) %all-reduce.5.cloned.1.call-update) | async-done | bytes 65552
  366.3 0.9 constant_dynamic-slice_fusion.10
  367.2 29.7 %all-reduce.1 = f32[64,4,32]{2,1,0:T(4,128)S(1)} all-reduce(f32[64,4,32]{2,1,0:T(4,128)S(1)} %constant_dynamic-slice_fusion.10), channel_id=7, replica_groups=mesh['groups'=2,'seq_0'=8,'seq_1'=8,'seq_2'=2] {'seq_0'}, use_global_device_ids=true, to_apply=%region_10.11.clone | all-reduce | flops 8192 | bytes 65536
  396.9 30.2 %all-reduce.2 = f32[8,4,32]{2,1,0:T(4,128)S(1)} all-reduce(f32[8,4,32]{2,1,0:T(4,128)S(1)} %constant_dynamic-slice_fusion.9), channel_id=8, replica_groups=mesh['groups'=2,'seq_0'=8,'seq_1'=8,'seq_2'=2] {'seq_1'}, use_global_device_ids=true, to_apply=%region_11.12.clone | all-reduce | flops 1024 | bytes 8192
  427.1 1.3 fusion.84
  (81 shorter events, 10.0 us)
Async XLA Ops:
  6.5 325.9 %copy-start = (bf16[1,384,4096]{2,1,0:T(8,128)(2,1)S(1)}, bf16[1,384,4096]{2,1,0:T(8,128)(2,1)}, u32[]{:S(2)}) copy-start(bf16[1,384,4096]{2,1,0:T(8,128)(2,1)} %param.25) | copy-start | bytes 9437188
  6.6 164.6 %all-gather.14.cloned.1.call-start = ((), (), s32[]{:S(2)}) async-start(), calls=%async_computation | async-start | bytes 1216512 | tf_op jit(solution)/shard_map/all_gather | solution.py:25
  131.5 85.4 %all-gather.16.cloned.1.call-start = ((), (), s32[]{:S(2)}) async-start(), calls=%async_computation.1 | async-start | bytes 1216512 | tf_op jit(solution)/shard_map/all_gather | solution.py:25
  176.9 148.4 %all-gather.18.cloned.1.call-start = ((), (), s32[]{:S(2)}) async-start(), calls=%async_computation.2 | async-start | bytes 8454144 | tf_op jit(solution)/shard_map/all_gather | solution.py:44
  224.1 18.3 %copy-start.2 = (f32[4,8]{1,0:T(4,128)S(1)}, f32[4,8]{1,0:T(4,128)}, u32[]{:S(2)}) copy-start(f32[4,8]{1,0:T(4,128)} %param.27) | copy-start | bytes 388
  224.1 18.5 %copy-start.3 = (s32[4,8]{1,0:T(4,128)S(1)}, s32[4,8]{1,0:T(4,128)}, u32[]{:S(2)}) copy-start(s32[4,8]{1,0:T(4,128)} %param.26) | copy-start | bytes 388
  242.2 124.1 %all-reduce.5.cloned.1.call-start = ((), (), s32[]{:S(2)}) async-start(), calls=%async_computation.3 | async-start | bytes 524288
  242.7 87.3 %copy-start.1 = (f32[4096]{0:T(1024)S(1)}, f32[4096]{0:T(1024)}, u32[]{:S(2)}) copy-start(f32[4096]{0:T(1024)} %param.22) | copy-start | bytes 49156
  332.4 4.4 %copy-start.6 = (u32[256]{0:T(256)S(1)}, u32[256]{0:T(256)}, u32[]{:S(2)}) copy-start(u32[256]{0:T(256)} %constant.103) | copy-start | bytes 3076
  332.5 5.0 %copy-start.5 = (u32[256]{0:T(256)S(1)}, u32[256]{0:T(256)}, u32[]{:S(2)}) copy-start(u32[256]{0:T(256)} %constant.107) | copy-start | bytes 3076
  332.5 5.5 %copy-start.4 = (u32[256]{0:T(256)S(1)}, u32[256]{0:T(256)}, u32[]{:S(2)}) copy-start(u32[256]{0:T(256)} %constant.111) | copy-start | bytes 3076
Sparse Core Ops, SparseCore 0:
  131.6 39.4 all-gather.13
  177.0 39.9 all-gather.15
  242.3 82.9 all-gather.17
  336.9 29.2 all-reduce.4
where the time goes:
time: 436 us; the launch traced here: 435 us
  waiting for transfers between devices  187 us (43%)
  blocking collectives  175 us (40%)
  local copies, waits for them, and re-layouts  22.7 us (5%)
  other arithmetic  22.4 us (5%)
  between operations  14.7 us (3%)
  matrix products  12.4 us (3%)
    all_gather x1, waiting for transfers between devices, over_pieces(): pieces = lax.all_gather(shard, axis)  82.5 us
    all_gather x2, waiting for transfers between devices, gathered_once(): both, at, found = (lax.all_gather(jnp.concatenate(lines), axis), 0, {})  77.6 us
    all_gather x1, blocking collectives, on_device(): whole_x = lax.all_gather(hidden_in, SEQ, axis=1, tiled=True)  62.8 us
    unnamed x2, blocking collectives  59.9 us
    all_gather x1, blocking collectives, on_device(): qkv_all = lax.all_gather(local_qkv, SEQ, axis=1, tiled=True)  50.7 us
    unnamed x5, waiting for transfers between devices  26.7 us
  transfers between devices with their start and end apart: 4, of which 4 were waited for; matrix products, arithmetic and copies ran while one was open for 1% of the time, Pallas kernels for 0%

commit v1 on v0

v1 whole, which is shorter than its diff:
```python
import functools
import math

import jax
import jax.numpy as jnp
import numpy as np
from jax import lax
from jax.experimental import pallas as pl
from jax.experimental.pallas import tpu as pltpu
from jax.sharding import Mesh
from jax.sharding import PartitionSpec as P

MESH = pl.DeviceIdType.MESH
BF = jnp.bfloat16
F32 = jnp.float32

HEADS = 64
KVH = 4
HD = 128
LANES = 128
SEQ = ("seq_0", "seq_1", "seq_2")
EPSILON = 1e-06
ROPE_BASE = 1000000.0


def kernel(
    nx, ny, nc,
    hid, in_gain, qkv_w, q_gain, k_hbm, v_hbm, lengths, out_w, post_gain,
    gate_w, up_w, down_w, ids, route, freq,
    out,
    ig, qw, kc, vc, ow, pg, gu, dw,
    b1s, b1, b2, xn, qk1s, qk1, qks, q2, qf,
    aos, ast, ao, asb, xo, xs, xob, xsb,
    ys, y1, y2s, y2, y3s, y3, res, pn, ms, m1, m2s, m2,
    wsem, ssem, rsem, qssem, qrsem,
):
    nrow = ny * nc
    x = lax.axis_index("seq_0")
    y = lax.axis_index("seq_1")
    c = lax.axis_index("seq_2")
    m = y * nc + c
    group_rows = nx // KVH
    g_me = x // group_rows
    dev = x * nrow + m
    block = (x % group_rows) * nrow + m
    seqs = hid.shape[0]
    width = hid.shape[1]
    qcols = qkv_w.shape[1]
    ctx = k_hbm.shape[1]
    half = gate_w.shape[2]
    nchunk = nx * nrow * width // LANES
    per_row = nchunk // nx
    share = LANES // width
    row_heads = nrow * qcols // HD
    per_group = HEADS // KVH

    def row_id(k):
        peer = lax.rem(m + k, nrow)
        return peer, {"seq_1": peer // nc, "seq_2": lax.rem(peer, nc)}

    def col_id(k):
        peer = lax.rem(x + k, nx)
        return peer, {"seq_0": peer}

    row_order = sorted(range(1, nrow), key=lambda k: -min(k, nrow - k))
    col_order = sorted(range(1, nx), key=lambda k: -min(k, nx - k))

    loads = [
        (in_gain, ig), (qkv_w, qw), (k_hbm, kc), (v_hbm, vc), (out_w, ow), (post_gain, pg),
        (gate_w.at[0], gu.at[:, pl.ds(0, half)]), (up_w.at[0], gu.at[:, pl.ds(half, half)]),
        (down_w.at[0], dw),
    ]
    loads = [pltpu.make_async_copy(s, d, wsem.at[n]) for n, (s, d) in enumerate(loads)]

    barrier = pltpu.get_barrier_semaphore()
    for k in row_order:
        pl.semaphore_signal(barrier, inc=1, device_id=row_id(k)[1], device_id_type=MESH)
    for k in col_order:
        pl.semaphore_signal(barrier, inc=1, device_id=col_id(k)[1], device_id_type=MESH)
    for load in loads:
        load.start()

    def send_row(src_of, dst, phase):
        for k in row_order:
            peer, where = row_id(k)
            pltpu.make_async_remote_copy(
                src_ref=src_of(peer), dst_ref=dst.at[m], send_sem=ssem.at[phase],
                recv_sem=rsem.at[phase], device_id=where, device_id_type=MESH,
            ).start()

    def send_col(src_of, dst, phase):
        for k in col_order:
            peer, where = col_id(k)
            pltpu.make_async_remote_copy(
                src_ref=src_of(peer), dst_ref=dst.at[x], send_sem=ssem.at[phase],
                recv_sem=rsem.at[phase], device_id=where, device_id_type=MESH,
            ).start()

    def whole(buf, phase):
        part = buf.at[pl.ds(0, buf.shape[0] - 1)]
        return pltpu.make_async_remote_copy(
            src_ref=part, dst_ref=part, send_sem=ssem.at[phase], recv_sem=rsem.at[phase],
            device_id=col_id(1)[1], device_id_type=MESH,
        )

    phases = []

    def received(buf, phase):
        phases.append((buf, phase))
        whole(buf, phase).wait_recv()

    hv = hid[...].astype(F32)
    lane = lax.broadcasted_iota(jnp.int32, (seqs, LANES), 1)
    own = jnp.where(lane // width == lax.rem(m, share), jnp.concatenate([hv] * share, axis=1), 0.0)
    b1s[...] = own.astype(BF)
    b1[m] = own.astype(BF)

    rows = lax.broadcasted_iota(jnp.int32, (seqs, LANES), 0)
    pos = jnp.zeros((seqs, LANES), jnp.int32)
    for s in range(seqs):
        pos = jnp.where(rows == s, lengths[s], pos)
    angle = pos.astype(F32) * freq[...]
    cosv = jnp.cos(angle)
    sinv = jnp.sin(angle)
    sinv = jnp.where(lane < HD // 2, -sinv, sinv)

    pl.semaphore_wait(barrier, nrow - 1 + nx - 1)

    send_row(lambda peer: b1s, b1, 0)
    received(b1, 0)
    for k in range(per_row):
        chunk = b1[share * k].astype(F32)
        for e in range(1, share):
            chunk = chunk + b1[share * k + e].astype(F32)
        b2[x, k] = chunk.astype(BF)
    send_col(lambda peer: b2.at[x], b2, 1)
    loads[0].wait()
    loads[1].wait()
    received(b2, 1)
    squares = jnp.zeros((seqs, LANES), F32)
    for n in range(nchunk):
        v = b2[n // per_row, n % per_row].astype(F32)
        squares = squares + v * v
    scale = lax.rsqrt(jnp.sum(squares, axis=1, keepdims=True) / (nchunk * LANES) + EPSILON)
    for n in range(nchunk):
        v = b2[n // per_row, n % per_row].astype(F32)
        xn[:, n * LANES : (n + 1) * LANES] = (v * scale * ig[n : n + 1, :]).astype(BF)
    qkv = jnp.dot(xn[...], qw[...], preferred_element_type=F32)
    qkv = qkv.astype(BF).astype(F32)
    shift = lax.rem(m * qcols, LANES)
    wide = jnp.concatenate([qkv, jnp.zeros((seqs, LANES - qcols), F32)], axis=1)
    wide = pltpu.roll(wide, shift, 1)
    first = jnp.where(lane >= shift, wide, 0.0).astype(BF)
    second = jnp.where(lane < shift, wide, 0.0).astype(BF)
    qk1s[0] = first
    qk1s[1] = second
    qk1[m, 0] = first
    qk1[m, 1] = second
    send_row(lambda peer: qk1s, qk1, 2)
    received(qk1, 2)
    for h in range(row_heads):
        acc = None
        for d in range(nrow):
            at = d * qcols // LANES
            for e in range(2):
                if at + e == h and (e == 0 or (d + 1) * qcols > (at + 1) * LANES):
                    piece = qk1[d, e].astype(F32)
                    acc = piece if acc is None else acc + piece
        head = row_heads * x + h
        is_q = head < HEADS
        is_v = head >= HEADS + KVH
        mean_sq = jnp.mean(acc * acc, axis=1, keepdims=True)
        gain = jnp.where(is_q, q_gain[...], 1.0)
        normed = acc * lax.rsqrt(mean_sq + EPSILON) * gain
        turned = normed * cosv + pltpu.roll(normed, HD // 2, 1) * sinv
        turned = turned * jnp.where(is_q, HD ** -0.5, 1.0)
        qks[h] = jnp.where(is_v, acc, turned).astype(BF)

    def head_sends(act):
        for h in range(row_heads):
            head = row_heads * x + h
            extra = head >= HEADS
            group = jnp.where(extra, lax.rem(head, KVH), head // per_group)
            slot = jnp.where(extra, per_group + (head - HEADS) // KVH, lax.rem(head, per_group))
            for e in range(group_rows):
                act(h, e, group_rows * group + e, slot)

    def head_start(h, e, target, slot):
        @pl.when(target != x)
        def _():
            pltpu.make_async_remote_copy(
                src_ref=qks.at[h], dst_ref=q2.at[slot], send_sem=qssem.at[h, e],
                recv_sem=qrsem.at[slot], device_id={"seq_0": target}, device_id_type=MESH,
            ).start()

        @pl.when(target == x)
        def _():
            q2[slot] = qks[h]

    def head_sent(h, e, target, slot):
        @pl.when(target != x)
        def _():
            pltpu.make_async_remote_copy(
                src_ref=qks.at[h], dst_ref=q2.at[slot], send_sem=qssem.at[h, e],
                recv_sem=qrsem.at[slot], device_id={"seq_0": target}, device_id_type=MESH,
            ).wait_send()

    def head_wait(slot):
        if slot < per_group:
            head = g_me * per_group + slot
        else:
            head = HEADS + (slot - per_group) * KVH + g_me

        @pl.when(head // row_heads != x)
        def _():
            pltpu.make_async_remote_copy(
                src_ref=qks.at[0], dst_ref=q2.at[slot], send_sem=qssem.at[0, 0],
                recv_sem=qrsem.at[slot], device_id=col_id(1)[1], device_id_type=MESH,
            ).wait_recv()

    head_sends(head_start)
    loads[2].wait()
    loads[3].wait()
    for slot in range(per_group):
        head_wait(slot)
    for j in range(per_group):
        qf[j] = q2[j].astype(F32)
    place = block * ctx + lax.broadcasted_iota(jnp.int32, (per_group, ctx), 1)
    states = []
    for s in range(seqs):
        qs = qf[:, s, :].astype(BF)
        scores = lax.dot_general(qs, kc[s], (((1,), (1,)), ((), ())), preferred_element_type=F32)
        live = place < lengths[s]
        scores = jnp.where(live, scores, -1e30)
        top = jnp.max(scores, axis=1, keepdims=True)
        probs = jnp.where(live, jnp.exp(scores - top), 0.0)
        total = jnp.sum(probs, axis=1, keepdims=True)
        part = jnp.dot(probs.astype(BF), vc[s], preferred_element_type=F32)
        states.append((qs, top, total, part))
    head_wait(per_group)
    head_wait(per_group + 1)
    tops, totals, parts = [], [], []
    for s, (qs, top, total, part) in enumerate(states):
        kn = q2[per_group].astype(F32)[s : s + 1, :]
        vn = q2[per_group + 1].astype(F32)[s : s + 1, :]
        score = jnp.sum(qs.astype(F32) * kn, axis=1, keepdims=True)
        score = jnp.where(block == 0, score, -1e30)
        high = jnp.maximum(top, score)
        keep = jnp.exp(top - high)
        mine = jnp.where(block == 0, jnp.exp(score - high), 0.0)
        tops.append(high)
        totals.append(keep * total + mine)
        parts.append(keep * part + mine * vn)
    wide_lane = lax.broadcasted_iota(jnp.int32, (seqs * per_group, LANES), 1)
    stat = jnp.where(wide_lane == 0, jnp.concatenate(tops, axis=0), jnp.concatenate(totals, axis=0))
    stat_t = stat.T[0:2]
    stat_t = jnp.concatenate([stat_t, stat_t], axis=1)
    part_t = jnp.concatenate(parts, axis=0).T
    pieces = HD // 16
    for q in range(pieces):
        both = [part_t[16 * q : 16 * q + 8], part_t[16 * q + 8 : 16 * q + 16]]
        aos[q] = jnp.concatenate(both, axis=1).astype(BF)
    ast[...] = stat_t
    asb[m] = stat_t
    send_row(lambda peer: ast, asb, 3)
    send_row(lambda peer: aos.at[lax.rem(peer, pieces)], ao, 4)
    ao[m] = aos[lax.rem(m, pieces)]
    received(asb, 3)
    received(ao, 4)

    def merged(stats, outs):
        top = functools.reduce(jnp.maximum, [t[0:1] for t in stats])
        total, acc = 0.0, 0.0
        for t, o in zip(stats, outs):
            w = jnp.exp(t[0:1] - top)
            total = total + w * t[1:2]
            acc = acc + w * o.astype(F32)
        return top, total, acc

    top, total, acc = merged([asb[d] for d in range(nrow)], [ao[d] for d in range(nrow)])
    st = jnp.concatenate([top, total], axis=0)
    xs[...] = st
    xo[...] = acc.astype(BF)
    xsb[x] = st
    xob[x] = acc.astype(BF)
    send_col(lambda peer: xs, xsb, 5)
    send_col(lambda peer: xo, xob, 6)
    loads[4].wait()
    received(xsb, 5)
    received(xob, 6)
    lines = []
    for g in range(KVH):
        span = range(g * group_rows, (g + 1) * group_rows)
        top, total, acc = merged([xsb[d] for d in span], [xob[d] for d in span])
        acc = acc / total
        lines += [acc, pltpu.roll(acc, LANES // 2, 1)]
    lines = jnp.concatenate(lines, axis=0).astype(BF)
    head = (nrow * x + m) // pieces
    pick_row = lax.broadcasted_iota(jnp.int32, (8, LANES), 0)
    pick_lane = lax.broadcasted_iota(jnp.int32, (8, LANES), 1)
    pick = jnp.where((pick_lane == per_group * pick_row + head) & (pick_row < seqs), 1.0, 0.0)
    attn = lax.dot_general(
        pick.astype(BF), lines, (((1,), (1,)), ((), ())), preferred_element_type=F32
    ).astype(BF)
    proj = jnp.dot(attn, ow[...].reshape(-1, ow.shape[2]), preferred_element_type=F32)
    for n in range(nchunk):
        ys[n] = proj[0:seqs, n * LANES : (n + 1) * LANES]
    per_dev = nchunk // nrow
    send_row(lambda peer: ys.at[pl.ds(peer * per_dev, per_dev)], y1, 7)
    y1[m] = ys[pl.ds(m * per_dev, per_dev)]
    received(y1, 7)
    total = y1[0]
    for d in range(1, nrow):
        total = total + y1[d]
    y2s[...] = total
    y2[x] = total
    send_col(lambda peer: y2s, y2, 8)
    received(y2, 8)
    total = y2[0]
    for d in range(1, nx):
        total = total + y2[d]
    y3s[...] = total
    y3[m] = total
    send_row(lambda peer: y3s, y3, 9)
    loads[5].wait()
    loads[6].wait()
    loads[7].wait()
    received(y3, 9)
    squares = jnp.zeros((seqs, LANES), F32)
    for n in range(nchunk):
        v = b2[n // per_row, n % per_row].astype(F32) + y3[n // per_dev, n % per_dev]
        res[n] = v
        squares = squares + v * v
    scale = lax.rsqrt(jnp.sum(squares, axis=1, keepdims=True) / (nchunk * LANES) + EPSILON)
    for n in range(nchunk):
        pn[:, n * LANES : (n + 1) * LANES] = (res[n] * scale * pg[n : n + 1, :]).astype(BF)
    both = jnp.dot(pn[...], gu[...], preferred_element_type=F32)
    gate_val, up_val = both[:, :half], both[:, half:]
    act = (gate_val / (1.0 + jnp.exp(-gate_val)) * up_val).astype(BF)
    loads[8].wait()
    slab = jnp.dot(act, dw[...], preferred_element_type=F32)
    routes = route[...]
    routes = routes / jnp.sum(routes, axis=1, keepdims=True)
    coef = jnp.sum(jnp.where(ids[...] == dev // 2, routes, 0.0), axis=1, keepdims=True)
    slab = slab * coef
    for n in range(nchunk):
        ms[n] = slab[:, n * LANES : (n + 1) * LANES]
    send_col(lambda peer: ms.at[pl.ds(peer * per_row, per_row)], m1, 10)
    m1[x] = ms[pl.ds(x * per_row, per_row)]
    received(m1, 10)
    total = m1[0]
    for d in range(1, nx):
        total = total + m1[d]
    m2s[...] = total
    send_row(lambda peer: m2s.at[peer // share], m2, 11)
    m2[m] = m2s[m // share]
    received(m2, 11)
    total = res[x * per_row + m // share]
    for d in range(nrow):
        total = total + m2[d]
    at = lax.rem(m, share)
    final = total[:, 0:width]
    for e in range(1, share):
        final = jnp.where(at == e, total[:, e * width : (e + 1) * width], final)
    out[...] = final
    head_sends(head_sent)
    for buf, phase in phases:
        whole(buf, phase).wait_send()


def on_device(
    hidden_in, in_gain, qkv_weight, q_gain, k_cache, v_cache, lengths, out_weight, post_gain,
    gate_weight, up_weight, down_weight, expert_ids, route_weight,
):
    nx, ny, nc = (lax.axis_size(a) for a in SEQ)
    nrow = ny * nc
    seqs, width = hidden_in.shape
    depth = in_gain.shape[0]
    qcols = qkv_weight.shape[1]
    half = gate_weight.shape[2]
    nchunk = depth // LANES
    row_heads = nrow * qcols // HD
    per_group = HEADS // KVH
    freq = ROPE_BASE ** (-2.0 * np.arange(HD // 2) / HD)
    freq = np.concatenate([freq, freq])[None, :].astype(np.float32)
    vm = lambda *shape, t=F32: pltpu.VMEM(shape, t)
    tile = (seqs, LANES)
    per_row, per_dev = nchunk // nx, nchunk // nrow
    scratch = [
        vm(nchunk, LANES), vm(depth, qcols, t=BF), vm(*k_cache.shape, t=BF),
        vm(*v_cache.shape, t=BF), vm(*out_weight.shape, t=BF), vm(nchunk, LANES),
        vm(depth, 2 * half, t=BF), vm(half, depth, t=BF),
        vm(*tile, t=BF), vm(nrow, *tile, t=BF), vm(nx, per_row, *tile, t=BF), vm(seqs, depth, t=BF),
        vm(2, *tile, t=BF), vm(nrow, 2, *tile, t=BF), vm(row_heads, *tile, t=BF),
        vm(per_group + 2, *tile, t=BF), vm(per_group, *tile),
        vm(HD // 16, 8, LANES, t=BF), vm(2, LANES), vm(nrow, 8, LANES, t=BF), vm(nrow, 2, LANES),
        vm(8, LANES, t=BF), vm(2, LANES), vm(nx, 8, LANES, t=BF), vm(nx, 2, LANES),
        vm(nchunk, *tile), vm(nrow, per_dev, *tile), vm(per_dev, *tile), vm(nx, per_dev, *tile),
        vm(per_dev, *tile), vm(nrow, per_dev, *tile), vm(nchunk, *tile), vm(seqs, depth, t=BF),
        vm(nchunk, *tile), vm(nx, per_row, *tile), vm(per_row, *tile), vm(nrow, *tile),
        pltpu.SemaphoreType.DMA((9,)), pltpu.SemaphoreType.DMA((12,)),
        pltpu.SemaphoreType.DMA((12,)), pltpu.SemaphoreType.DMA((row_heads, nx // KVH)),
        pltpu.SemaphoreType.DMA((per_group + 2,)),
    ]
    hbm = pl.BlockSpec(memory_space=pl.ANY)
    vmem = pl.BlockSpec(memory_space=pltpu.VMEM)
    smem = pl.BlockSpec(memory_space=pltpu.SMEM)
    return pl.pallas_call(
        functools.partial(kernel, nx, ny, nc),
        out_shape=jax.ShapeDtypeStruct((seqs, width), F32),
        in_specs=[vmem, hbm, hbm, vmem, hbm, hbm, smem, hbm, hbm, hbm, hbm, hbm, vmem, vmem, vmem],
        out_specs=vmem,
        scratch_shapes=scratch,
        compiler_params=pltpu.CompilerParams(
            collective_id=0, has_side_effects=True, vmem_limit_bytes=48 * 1024 * 1024
        ),
    )(
        hidden_in, in_gain.reshape(nchunk, LANES), qkv_weight, q_gain.reshape(1, HD), k_cache,
        v_cache, lengths, out_weight, post_gain.reshape(nchunk, LANES), gate_weight, up_weight,
        down_weight, expert_ids, route_weight, jnp.asarray(freq),
    )


def solution(mesh):
    split = Mesh(
        mesh.devices.reshape(mesh.shape["groups"], 8, 8, 2), ("groups", "seq_0", "seq_1", "seq_2")
    )
    placed = (
        P("groups", SEQ),
        P(),
        P(None, SEQ),
        P(),
        P("groups", SEQ, None),
        P("groups", SEQ, None),
        P("groups"),
        P(None, SEQ, None),
        P(),
        P(SEQ, None, None),
        P(SEQ, None, None),
        P(SEQ, None, None),
        P("groups", None),
        P("groups", None),
    )
    return jax.shard_map(
        on_device, mesh=split, in_specs=placed, out_specs=P("groups", SEQ), check_vma=False
    )
```

time: 436 us -> 89.9 us (0.21)
  the two profiles are of different devices: /device:TPU:516 before, /device:TPU:513 now
where the time goes in v1:
time: 89.9 us; the launch traced here: 89.5 us
  Pallas kernels  78.4 us (87%)
  local copies, waits for them, and re-layouts  11 us (12%)
    pallas_call x1, Pallas kernels, on_device(): pl.pallas_call(functools.partial(kernel, nx, ny, nc), out_shape=jax.Shape...  78.4 us
    unnamed x24, local copies, waits for them, and re-layouts  11 us

profile of v1, /device:TPU:513, one launch (start us, length us, event | category | flops | bytes accessed | tf_op | source)
XLA Modules:
  0.0 89.5 jit_solution(13485236880333488598)
XLA Ops:
  0.0 1.5 %copy.16.qkv_w = bf16[4096,72]{1,0:T(8,128)(2,1)S(1)} copy(bf16[4096,72]{0,1:T(8,128)(2,1)} %param.17) | data formatting | bytes 1179648 | tf_op args[2]
  1.5 0.0 copy-start
  1.6 1.2 %copy-done = bf16[4,1024,128]{2,1,0:T(8,128)(2,1)S(1)} copy-done((bf16[4,1024,128]{2,1,0:T(8,128)(2,1)S(1)}, bf16[4,1024,128]{2,1,0:T(8,128)(2,1)}, u32[]{:S(2)}) %copy-start) | copy-done | bytes 1048600
  2.8 0.0 copy-start.1
  2.8 1.2 %copy-done.1 = bf16[4,1024,128]{2,1,0:T(8,128)(2,1)S(1)} copy-done((bf16[4,1024,128]{2,1,0:T(8,128)(2,1)S(1)}, bf16[4,1024,128]{2,1,0:T(8,128)(2,1)}, u32[]{:S(2)}) %copy-start.1) | copy-done | bytes 1048600
  4.0 0.0 copy-start.2
  4.0 1.0 %copy-done.2 = bf16[4,16,4096]{2,1,0:T(8,128)(2,1)S(1)} copy-done((bf16[4,16,4096]{2,1,0:T(8,128)(2,1)S(1)}, bf16[4,16,4096]{2,1,0:T(8,128)(2,1)}, u32[]{:S(2)}) %copy-start.2) | copy-done | bytes 524312
  5.0 0.0 copy-start.3
  5.0 0.7 copy-done.3
  5.8 0.0 copy-start.4
  5.8 0.7 copy-done.4
  6.5 0.0 copy-start.5
  6.5 0.7 copy-done.5
  7.2 0.0 copy-start.6
  7.2 0.7 copy-done.6
  7.8 0.0 copy-start.7
  7.8 0.7 copy-done.7
  8.5 0.0 copy-start.8
  8.5 0.7 copy-done.8
  9.2 0.0 copy-start.9
  9.2 0.7 copy-done.9
  9.8 0.0 copy-start.10
  9.8 0.7 copy-done.10
  10.5 78.4 %shard_map.145 = f32[4,32]{1,0:T(4,128)S(1)} custom-call(bf16[4,32]{1,0:T(4,128)(2,1)S(1)} %copy-done.7, f32[32,128]{1,0:T(8,128)S(1)} %bitcast.3, bf16[4096,72]{1,0:T(8,128)(2,1)S(1)} %copy.16.qkv_w, f32[1,128]{1,0:T(1,128)S(1)} %bitcast.5, bf16[4,1024,128]{2,1,0:T(8,128)(2,1)S(1)} %copy-done, bf16[4,1024,128]{2,1,0:T(8,128)(2,1)S(1)} %copy-done.1, ...), custom_call_target="tpu_custom_call" | custom-call | tf_op jit(solution)/shard_map/pallas_call | solution.py:408
  88.9 0.6 copy.18
Async XLA Ops:
  1.5 1.2 %copy-start = (bf16[4,1024,128]{2,1,0:T(8,128)(2,1)S(1)}, bf16[4,1024,128]{2,1,0:T(8,128)(2,1)}, u32[]{:S(2)}) copy-start(bf16[4,1024,128]{2,1,0:T(8,128)(2,1)} %k_hbm.1) | copy-start | bytes 3145732
  2.8 1.2 %copy-start.1 = (bf16[4,1024,128]{2,1,0:T(8,128)(2,1)S(1)}, bf16[4,1024,128]{2,1,0:T(8,128)(2,1)}, u32[]{:S(2)}) copy-start(bf16[4,1024,128]{2,1,0:T(8,128)(2,1)} %v_hbm.1) | copy-start | bytes 3145732
  4.0 1.0 %copy-start.2 = (bf16[4,16,4096]{2,1,0:T(8,128)(2,1)S(1)}, bf16[4,16,4096]{2,1,0:T(8,128)(2,1)}, u32[]{:S(2)}) copy-start(bf16[4,16,4096]{2,1,0:T(8,128)(2,1)} %out_w.1) | copy-start | bytes 1572868
  5.0 0.7 copy-start.3
  5.8 0.7 copy-start.4
  6.5 0.7 copy-start.5
  7.2 0.7 copy-start.6
  7.8 0.7 copy-start.7
  8.5 0.7 copy-start.8
  9.2 0.7 copy-start.9
  9.8 0.7 copy-start.10
